TPU v7x, 32 devices: a whole 2x2x4 slice. The times are simulated.
32 devices in a mesh: dp: 8 (over y, x, core), tensor: 4 (over z).
Axes of the slice: x: 2, y: 2, z: 4, core: 2. Of those that a mesh axis runs over, the one named last changes fastest.
Arguments:
- attn_out: bfloat16 [3072, 4096], P('dp', 'tensor'), may hold values from -24 to 24
- out_grad: bfloat16 [3072, 4096], P('dp', 'tensor'), may hold values from -6 to 6
- proj_in: bfloat16 [64, 4096], P(None, 'tensor'), may hold values from -0.09375 to 0.09375
- proj_out: bfloat16 [64, 4096], P(None, 'tensor'), may hold values from -0.09375 to 0.09375
- targets: float32 [256, 64, 64], P(None, 'tensor'), may hold values from -6 to 6
Outputs:
- scores: float32 [48, 256], P('dp')
All inputs are finite; a program needn't handle non-finite values.
Results may differ from a plain program's by a relative error of at most 0.0015.
Values sent between devices are 32-bit elements; how exact they have to be, the bound alone decides.
A program may use at most 64 MiB of HBM per device.

v0:
```python
import jax
import jax.numpy as jnp
from jax import lax
from jax.sharding import PartitionSpec as P

LEN = 64
damping_ratio = 0.5
epsilon = 1e-06


def inner_rows(left, right):
    return lax.dot_general(
        left,
        right,
        (((1,), (1,)), ((), ())),
        precision=lax.Precision.HIGHEST,
        preferred_element_type=jnp.float32,
    )


def shards(attn_out, out_grad, proj_in, proj_out, targets):
    tok_rows = attn_out.shape[0]
    proj_rank = proj_in.shape[0]
    seq_count = tok_rows // LEN
    inputs_part = jnp.einsum("td,rd->tr", attn_out, proj_in, preferred_element_type=jnp.float32)
    grads_part = jnp.einsum("td,rd->tr", out_grad, proj_out, preferred_element_type=jnp.float32)
    inputs_low = lax.psum_scatter(inputs_part, "tensor", scatter_dimension=1, tiled=True)
    grads_low = lax.psum(grads_part, "tensor")
    part_width = inputs_low.shape[1]
    sample_grads = jnp.einsum(
        "sti,sto->sio",
        inputs_low.reshape(seq_count, LEN, part_width),
        grads_low.reshape(seq_count, LEN, proj_rank),
        precision=lax.Precision.HIGHEST,
    ).reshape(seq_count, part_width * proj_rank)
    target_rows = targets.reshape(targets.shape[0], part_width * proj_rank)
    gathered = lax.all_gather(sample_grads, "dp", axis=0, tiled=True)
    gram_matrix = inner_rows(gathered, gathered)
    cross_terms = inner_rows(gathered, target_rows)
    gram_matrix, cross_terms = lax.psum((gram_matrix, cross_terms), "tensor")
    trace_sum = jnp.trace(gram_matrix)
    samples = gram_matrix.shape[0]
    damping = damping_ratio * trace_sum / (samples * proj_rank * proj_rank) + epsilon
    system = gram_matrix / samples + damping * jnp.eye(samples, dtype=jnp.float32)
    factor = jnp.linalg.cholesky(system)
    solved = jax.scipy.linalg.cho_solve((factor, True), cross_terms)
    return lax.dynamic_slice_in_dim(solved, lax.axis_index("dp") * seq_count, seq_count, 0)


def solution(mesh):
    in_specs = (
        P("dp", "tensor"),
        P("dp", "tensor"),
        P(None, "tensor"),
        P(None, "tensor"),
        P(None, "tensor", None),
    )
    out_specs = P("dp", None)
    return jax.shard_map(shards, mesh=mesh, in_specs=in_specs, out_specs=out_specs, check_vma=False)
```

profile of v0, /device:TPU:0, one launch (start us, length us, event | category | flops | bytes accessed | tf_op | source)
XLA Modules:
  0.0 116.2 jit_solution(16831811706130720864)
XLA Ops:
  6.5 0.0 copy-start
  6.5 0.0 copy-start.1
  6.5 0.0 reduce-scatter.2.cloned.1.call-start
  6.5 0.0 copy-start.2
  6.5 2.3 %fusion.8 = f32[384,64]{0,1:T(8,128)} fusion(bf16[384,1024]{1,0:T(8,128)(2,1)} %param.5, bf16[64,1024]{1,0:T(8,128)(2,1)} %param.7), kind=kOutput, calls=%fused_computation.17 | convolution fusion | flops 50331648 | bytes 1015808 | tf_op jit(solution)/shard_map/td,rd->tr/dot_general | solution.py:25
  8.8 0.0 reduce-scatter.2.cloned.1.call-update
  8.8 0.0 all-reduce.3.cloned.1.call-start
  8.9 0.0 copy-done.1
  8.9 0.0 copy-done.2
  8.9 1.0 fusion.9
  9.9 0.0 all-reduce.3.cloned.1.call-update
  10.0 21.8 %reduce-scatter.2.cloned.1.call-done = f32[384,16]{0,1:T(8,128)} async-done(((f32[384,64]{0,1:T(8,128)}), f32[384,16]{0,1:T(8,128)}) %reduce-scatter.2.cloned.1.call-update) | async-done | bytes 24592 | tf_op jit(solution)/shard_map/reduce_scatter | solution.py:27
  31.7 0.8 reshape.25
  32.6 34.7 %all-reduce.3.cloned.1.call-done = f32[6,64,64]{2,1,0:T(8,128)} async-done(((f32[6,64,64]{2,1,0:T(8,128)}), f32[6,64,64]{2,1,0:T(8,128)}) %all-reduce.3.cloned.1.call-update) | async-done | bytes 98320 | tf_op jit(solution)/shard_map/psum | solution.py:28
  67.2 1.2 %fusion = f32[6,16,64]{2,1,0:T(8,128)S(1)} fusion(f32[6,64,64]{2,1,0:T(8,128)} %all-reduce.3.cloned.1.call-done, f32[6,64,16]{1,0,2:T(8,128)S(1)} %reshape.25), kind=kOutput, calls=%fused_computation | convolution fusion | flops 4718592 | bytes 147456 | tf_op jit(solution)/shard_map/sti,sto->sio/dot_general | solution.py:30
  68.5 0.1 reshape.29
  68.5 9.2 %all-gather = f32[8,6,1024]{2,1,0:T(8,128)S(1)} all-gather(f32[1,6,1024]{2,1,0:T(8,128)S(1)} %reshape.29), channel_id=1, replica_groups=mesh['dp'=8,'tensor'=4] {'dp'}, dimensions={0}, use_global_device_ids=true | all-gather | bytes 221184 | tf_op jit(solution)/shard_map/all_gather | solution.py:37
  77.7 0.3 fusion.10
  78.1 0.0 copy-done
  78.1 0.6 fusion.11
  78.7 18.8 %all-reduce = (f32[48,256]{1,0:T(8,128)S(1)}, f32[48,48]{1,0:T(8,128)S(1)}) all-reduce(f32[48,256]{1,0:T(8,128)S(1)} %fusion.11, f32[48,48]{1,0:T(8,128)S(1)} %fusion.10), channel_id=1, replica_groups=mesh['dp'=8,'tensor'=4] {'tensor'}, use_global_device_ids=true, to_apply=%region_6.7 | all-reduce | flops 14592 | bytes 116736 | tf_op jit(solution)/shard_map/psum | solution.py:40
  97.5 0.6 select_reduce_fusion.1
  98.8 0.1 copy.14
  98.9 4.4 %cholesky.17 = f32[48,48]{1,0:T(8,128)S(1)} custom-call(f32[48,48]{1,0:T(8,128)S(1)} %fusion.7), custom_call_target="Cholesky" | custom-call | tf_op jit(solution)/shard_map/jit(cholesky)/cholesky | solution.py:45
  103.3 0.6 compare_reduce_fusion
  103.9 0.7 fusion.2
  104.6 3.7 %custom-call.10 = f32[1,48,48]{1,2,0:T(8,128)S(1)} custom-call(f32[1,48,48]{2,1,0:T(8,128)S(1)} %fusion.2), custom_call_target="InvertDiagBlocksLowerTriangular" | custom-call | tf_op jit(solution)/shard_map/jit(_cho_solve)/triangular_solve | solution.py:46
  108.3 0.2 fusion.5
  108.5 0.2 fusion.3
  108.7 0.6 constant_dynamic-slice_fusion
  (4 shorter events, 0.1 us)
Async XLA Ops:
  6.5 71.5 %copy-start = (f32[256,16,64]{0,2,1:T(8,128)S(1)}, f32[256,16,64]{0,2,1:T(8,128)}, u32[]{:S(2)}) copy-start(f32[256,16,64]{0,2,1:T(8,128)} %param.9) | copy-start | bytes 3145732
  6.5 2.4 %copy-start.1 = (bf16[384,1024]{1,0:T(8,128)(2,1)S(1)}, bf16[384,1024]{1,0:T(8,128)(2,1)}, u32[]{:S(2)}) copy-start(bf16[384,1024]{1,0:T(8,128)(2,1)} %param.6) | copy-start | bytes 2359300
  6.5 25.2 %reduce-scatter.2.cloned.1.call-start = ((), (), s32[]{:S(2)}) async-start(), calls=%async_computation.1 | async-start | bytes 122880 | tf_op jit(solution)/shard_map/reduce_scatter | solution.py:27
  6.5 2.4 %copy-start.2 = (bf16[64,1024]{1,0:T(8,128)(2,1)S(1)}, bf16[64,1024]{1,0:T(8,128)(2,1)}, u32[]{:S(2)}) copy-start(bf16[64,1024]{1,0:T(8,128)(2,1)} %param.8) | copy-start | bytes 393220
  8.8 58.4 %all-reduce.3.cloned.1.call-start = ((), (), s32[]{:S(2)}) async-start(), calls=%async_computation.2 | async-start | bytes 393216 | tf_op jit(solution)/shard_map/psum | solution.py:28
Sparse Core Ops, SparseCore 0:
  9.6 22.1 reduce-scatter.1
  34.1 33.1 all-reduce.2
where the time goes:
time: 116 us
  waiting for transfers between devices  56.5 us (49%)
  blocking collectives  28 us (24%)
  between operations  14.2 us (12%)
  other arithmetic  10 us (9%)
  matrix products  5.86 us (5%)
  local copies, waits for them, and re-layouts  1.62 us (1%)
    psum x1, waiting for transfers between devices, shards(): grads_low = lax.psum(grads_part, 'tensor')  34.7 us
    reduce_scatter x1, waiting for transfers between devices, shards(): lax.psum_scatter(inputs_part, 'tensor', scatter_dimension=1, tiled=True)  21.8 us
    psum x1, blocking collectives, shards(): gram_matrix, cross_terms = lax.psum((gram_matrix, cross_terms), 'tensor')  18.8 us
    all_gather x1, blocking collectives, shards(): gathered = lax.all_gather(sample_grads, 'dp', axis=0, tiled=True)  9.17 us
    another operation x3, other arithmetic, shards(): factor = jnp.linalg.cholesky(system)  5.05 us
    another operation x2, other arithmetic, shards(): solved = jax.scipy.linalg.cho_solve((factor, True), cross_terms)  4.32 us
  transfers between devices with their start and end apart: 2, of which 2 were waited for; matrix products, arithmetic and copies ran while one was open for 2% of the time, Pallas kernels for 0%

commit v1 on v0

--- a/solution.py
+++ b/solution.py
@@ -25,7 +25,8 @@
     inputs_part = jnp.einsum("td,rd->tr", attn_out, proj_in, preferred_element_type=jnp.float32)
     grads_part = jnp.einsum("td,rd->tr", out_grad, proj_out, preferred_element_type=jnp.float32)
     inputs_low = lax.psum_scatter(inputs_part, "tensor", scatter_dimension=1, tiled=True)
-    grads_low = lax.psum(grads_part, "tensor")
+    parts = lax.all_gather(grads_part, "tensor")
+    grads_low = jnp.sum(parts, axis=0)
     part_width = inputs_low.shape[1]
     sample_grads = jnp.einsum(
         "sti,sto->sio",

time: 116 us -> 79.5 us (0.69)
  waiting for transfers between devices: 56.5 us -> 5.22 us
  blocking collectives: 28 us -> 43.5 us
  matrix products: 5.86 us -> 4.24 us
    psum x1 -> x0, waiting for transfers between devices: 34.7 us -> none  [shards(): grads_low = lax.psum(grads_part, 'tensor')]
    all_gather x0 -> x1, blocking collectives: none -> 16.9 us  [shards(): parts = lax.all_gather(grads_part, 'tensor')]
    reduce_scatter x1, waiting for transfers between devices: 21.8 us -> 5.2 us  [shards(): lax.psum_scatter(inputs_part, 'tensor', scatter_dimension=1, tiled=True)]
    psum x1, blocking collectives: 18.8 us -> 17.4 us  [shards(): gram_matrix, cross_terms = lax.psum((gram_matrix, cross_terms), 'tensor')]
  transfers between devices with their start and end apart: 2 -> 1, of which waited for: 2 -> 1; matrix products, arithmetic and copies ran while one was open for 2% -> 1% of each run, Pallas kernels for 0% -> 0%
where the time goes in v1:
time: 79.5 us; the launch traced here: 79.2 us
  blocking collectives  43.5 us (55%)
  between operations  14.2 us (18%)
  other arithmetic  10.2 us (13%)
  waiting for transfers between devices  5.22 us (7%)
  matrix products  4.24 us (5%)
  local copies, waits for them, and re-layouts  1.88 us (2%)
    psum x1, blocking collectives, shards(): gram_matrix, cross_terms = lax.psum((gram_matrix, cross_terms), 'tensor')  17.4 us
    all_gather x1, blocking collectives, shards(): parts = lax.all_gather(grads_part, 'tensor')  16.9 us
    all_gather x1, blocking collectives, shards(): gathered = lax.all_gather(sample_grads, 'dp', axis=0, tiled=True)  9.2 us
    reduce_scatter x1, waiting for transfers between devices, shards(): lax.psum_scatter(inputs_part, 'tensor', scatter_dimension=1, tiled=True)  5.2 us
    another operation x3, other arithmetic, shards(): factor = jnp.linalg.cholesky(system)  5.05 us
    another operation x2, other arithmetic, shards(): solved = jax.scipy.linalg.cho_solve((factor, True), cross_terms)  4.32 us
    dot_general x1, matrix products, shards(): jnp.einsum('td,rd->tr', attn_out, proj_in, preferred_element_type=jnp.flo...  2.26 us
  transfers between devices with their start and end apart: 1, of which 1 were waited for; matrix products, arithmetic and copies ran while one was open for 1% of the time, Pallas kernels for 0%

profile of v1, /device:TPU:0, one launch (start us, length us, event | category | flops | bytes accessed | tf_op | source)
XLA Modules:
  0.0 79.2 jit_solution(11738905890525213787)
XLA Ops:
  6.5 0.0 copy-start
  6.5 0.0 copy-start.1
  6.5 0.0 reduce-scatter.2.cloned.1.call-start
  6.5 0.0 copy-start.2
  6.5 2.3 %fusion.8 = f32[384,64]{0,1:T(8,128)} fusion(bf16[384,1024]{1,0:T(8,128)(2,1)} %param.5, bf16[64,1024]{1,0:T(8,128)(2,1)} %param.7), kind=kOutput, calls=%fused_computation.17 | convolution fusion | flops 50331648 | bytes 1015808 | tf_op jit(solution)/shard_map/td,rd->tr/dot_general | solution.py:25
  8.8 0.0 reduce-scatter.2.cloned.1.call-update
  8.8 0.0 copy-done.1
  8.8 0.0 copy-done.2
  8.9 0.4 fusion.9
  9.2 16.9 %all-gather = f32[1536,64]{0,1:T(8,128)S(1)} all-gather(f32[384,64]{0,1:T(8,128)S(1)} %fusion.9), channel_id=2, replica_groups=mesh['dp'=8,'tensor'=4] {'tensor'}, dimensions={0}, use_global_device_ids=true | all-gather | bytes 491520 | tf_op jit(solution)/shard_map/all_gather | solution.py:28
  26.1 0.1 reshape.29
  26.2 0.2 reduce_sum.19
  26.5 0.1 copy.16
  26.6 5.2 %reduce-scatter.2.cloned.1.call-done = f32[384,16]{0,1:T(8,128)} async-done(((f32[384,64]{0,1:T(8,128)}), f32[384,16]{0,1:T(8,128)}) %reduce-scatter.2.cloned.1.call-update) | async-done | bytes 24592 | tf_op jit(solution)/shard_map/reduce_scatter | solution.py:27
  31.8 0.8 %reshape.25 = f32[6,64,16]{1,0,2:T(8,128)S(1)} reshape(f32[384,16]{0,1:T(8,128)} %reduce-scatter.2.cloned.1.call-done) | data formatting | bytes 49152 | tf_op jit(solution)/shard_map/reshape | solution.py:33
  32.6 0.3 fusion
  32.9 0.1 reshape.30
  33.0 9.2 %all-gather.1 = f32[8,6,1024]{2,1,0:T(8,128)S(1)} all-gather(f32[1,6,1024]{2,1,0:T(8,128)S(1)} %reshape.30), channel_id=1, replica_groups=mesh['dp'=8,'tensor'=4] {'dp'}, dimensions={0}, use_global_device_ids=true | all-gather | bytes 221184 | tf_op jit(solution)/shard_map/all_gather | solution.py:38
  42.2 0.3 fusion.10
  42.5 0.0 copy-done
  42.5 0.6 fusion.11
  43.2 17.4 %all-reduce = (f32[48,256]{1,0:T(8,128)S(1)}, f32[48,48]{1,0:T(8,128)S(1)}) all-reduce(f32[48,256]{1,0:T(8,128)S(1)} %fusion.11, f32[48,48]{1,0:T(8,128)S(1)} %fusion.10), channel_id=1, replica_groups=mesh['dp'=8,'tensor'=4] {'tensor'}, use_global_device_ids=true, to_apply=%region_6.7 | all-reduce | flops 14592 | bytes 116736 | tf_op jit(solution)/shard_map/psum | solution.py:41
  60.6 0.6 select_reduce_fusion.1
  61.8 0.1 copy.15
  61.9 4.4 %cholesky.17 = f32[48,48]{1,0:T(8,128)S(1)} custom-call(f32[48,48]{1,0:T(8,128)S(1)} %fusion.7), custom_call_target="Cholesky" | custom-call | tf_op jit(solution)/shard_map/jit(cholesky)/cholesky | solution.py:46
  66.4 0.6 compare_reduce_fusion
  67.0 0.7 fusion.2
  67.7 3.7 %custom-call.10 = f32[1,48,48]{1,2,0:T(8,128)S(1)} custom-call(f32[1,48,48]{2,1,0:T(8,128)S(1)} %fusion.2), custom_call_target="InvertDiagBlocksLowerTriangular" | custom-call | tf_op jit(solution)/shard_map/jit(_cho_solve)/triangular_solve | solution.py:47
  71.3 0.2 fusion.5
  71.6 0.2 fusion.3
  71.8 0.6 constant_dynamic-slice_fusion
  (4 shorter events, 0.1 us)
Async XLA Ops:
  6.5 36.0 %copy-start = (f32[256,16,64]{0,2,1:T(8,128)S(1)}, f32[256,16,64]{0,2,1:T(8,128)}, u32[]{:S(2)}) copy-start(f32[256,16,64]{0,2,1:T(8,128)} %param.9) | copy-start | bytes 3145732
  6.5 2.3 %copy-start.1 = (bf16[384,1024]{1,0:T(8,128)(2,1)S(1)}, bf16[384,1024]{1,0:T(8,128)(2,1)}, u32[]{:S(2)}) copy-start(bf16[384,1024]{1,0:T(8,128)(2,1)} %param.6) | copy-start | bytes 2359300
  6.5 25.3 %reduce-scatter.2.cloned.1.call-start = ((), (), s32[]{:S(2)}) async-start(), calls=%async_computation.1 | async-start | bytes 122880 | tf_op jit(solution)/shard_map/reduce_scatter | solution.py:27
  6.5 2.3 %copy-start.2 = (bf16[64,1024]{1,0:T(8,128)(2,1)S(1)}, bf16[64,1024]{1,0:T(8,128)(2,1)}, u32[]{:S(2)}) copy-start(bf16[64,1024]{1,0:T(8,128)(2,1)} %param.8) | copy-start | bytes 393220
Sparse Core Ops, SparseCore 0:
  9.6 22.1 reduce-scatter.1
